TPU v7x, 1024 devices: a whole 4x4x32 slice. The times are simulated.
1024 devices in a mesh: gx: 16 (over z_lo), gy: 8 (over z_hi, y), gz: 8 (over x, core).
Axes of the slice: x: 4, y: 4, z: 32 (z_hi: 2, z_lo: 16; z = z_hi * 16 + z_lo), core: 2. Of those that a mesh axis runs over, the one named last changes fastest.
Arguments:
- tokens: bfloat16 [1024, 4096], P(('gy', 'gz'), 'gx'), may hold values from -6 to 6
- expert_ids: int32 [1024, 2], P(('gy', 'gz')), may hold values from 0 to 7, all different within a row; in each aligned block of 16 rows (0 to 15, 16 to 31, ...) at most 8 rows name the same one
- gate_probs: float32 [1024, 2], P(('gy', 'gz')), may hold values from 0.2 to 1
- gate_weight: bfloat16 [8, 4096, 16384], P('gy', None, ('gz', 'gx')), may hold values from -0.09375 to 0.09375
- up_weight: bfloat16 [8, 4096, 16384], P('gy', None, ('gz', 'gx')), may hold values from -0.09375 to 0.09375
- down_weight: bfloat16 [8, 16384, 4096], P('gy', 'gz', 'gx'), may hold values from -0.046875 to 0.046875
Outputs:
- moe_output: bfloat16 [1024, 4096], P(('gy', 'gz'), 'gx')
Inputs may be any that keep to these rules, and one draw needn't show every extreme that they name: `expert_ids`: A token's two ids differ. Within each aligned block of 16 tokens no expert is named more than 8 times, and in some blocks one expert is named exactly 8 times.
All inputs are finite; a program needn't handle non-finite values.
Results may differ from a plain program's by a relative error of at most 0.0049.
Values may be sent and summed in bfloat16 or wider, within the bound.
No kernel may reach another device: no remote copies, remote signals or barrier semaphores. Data moves between devices by JAX's collectives and lax.ppermute only.
A program may use at most 32 MiB of HBM per device.

v0:
```python
import jax
import jax.numpy as jnp
from jax import lax
from jax.sharding import PartitionSpec as P

EXPERTS = 8
CAP = 8


def sent_to_all(value, axis):
    count = lax.axis_size(axis)
    return lax.all_to_all(
        jnp.broadcast_to(value[None], (count, *value.shape)), axis, 0, 0, tiled=True
    )


def joined_along(parts, dim):
    parts = jnp.moveaxis(parts, 0, dim)
    shape = parts.shape
    return parts.reshape(*shape[:dim], shape[dim] * shape[dim + 1], *shape[dim + 2 :])


def gather_directly(value, axis, dim):
    parts = sent_to_all(value, axis)
    return joined_along(parts, dim)


def in_blocks(value, dim, count):
    shape = value.shape
    parts = value.reshape(*shape[:dim], count, shape[dim] // count, *shape[dim + 1 :])
    return jnp.moveaxis(parts, dim, 0)


def sum_at_owner(value, axis, dim):
    parts = in_blocks(value, dim, lax.axis_size(axis))
    arrived = lax.all_to_all(parts, axis, split_axis=0, concat_axis=0, tiled=True)
    return arrived.sum(axis=0)


def route_tables(expert_ids, gate_probs, experts, capacity):
    token_count = expert_ids.shape[0]
    flattened = expert_ids.reshape(token_count * 2)
    labels = jnp.arange(experts, dtype=jnp.int32)
    onehot = (flattened[:, None] == labels[None, :]).astype(jnp.int32)
    before = jnp.cumsum(onehot, axis=0) - onehot
    slot_index = jnp.sum(before * onehot, axis=1)
    places = flattened * capacity + slot_index
    columns = jnp.arange(experts * capacity, dtype=jnp.int32)
    matches = (places[:, None] == columns[None, :]).astype(jnp.float32)
    matches = matches.reshape(token_count, 2, experts * capacity)
    picker = jnp.sum(matches, axis=1)
    combine_table = jnp.sum(matches * gate_probs[:, :, None], axis=1)
    return (picker, combine_table)


def body(tokens, expert_ids, gate_probs, gate_weight, up_weight, down_weight):
    size_gy = lax.axis_size("gy")
    size_gz = lax.axis_size("gz")
    local_experts = gate_weight.shape[0]
    hidden_cols = gate_weight.shape[2]
    picker, combine_table = route_tables(expert_ids, gate_probs, EXPERTS, CAP)
    selector = picker.astype(jnp.bfloat16)
    full_rows = gather_directly(tokens, "gx", 1)
    feature_width = full_rows.shape[1]
    buffer = jnp.einsum(
        "tr,tf->rf", selector, full_rows, preferred_element_type=jnp.float32
    ).astype(jnp.bfloat16)
    outgoing = buffer.reshape(size_gy, local_experts, CAP, feature_width).transpose(1, 0, 2, 3)[
        :, :, None
    ]
    arrived = lax.all_to_all(outgoing, "gy", split_axis=1, concat_axis=1, tiled=True)
    portion = lax.all_gather(arrived, "gz", axis=2, tiled=True)
    gate_part = jnp.einsum(
        "jyscd,jdh->jysch", portion, gate_weight, preferred_element_type=jnp.float32
    )
    up_part = jnp.einsum("jyscd,jdh->jysch", portion, up_weight, preferred_element_type=jnp.float32)
    stacked = jnp.concatenate([gate_part, up_part], axis=4)
    gate_act = stacked[..., :hidden_cols].reshape(local_experts, -1, hidden_cols)
    up_act = stacked[..., hidden_cols:].reshape(local_experts, -1, hidden_cols)
    hidden = (jax.nn.silu(gate_act) * up_act).astype(jnp.bfloat16)
    result_width = down_weight.shape[2]
    partial_out = jnp.einsum(
        "jrh,jhf->jrf",
        lax.all_gather(hidden, "gx", axis=2, tiled=True),
        down_weight,
        preferred_element_type=jnp.float32,
    )
    regrouped = partial_out.reshape(local_experts, size_gy, size_gz, CAP, result_width)
    summed = sum_at_owner(regrouped, "gz", 2)
    returned = lax.all_to_all(summed, "gy", split_axis=1, concat_axis=1, tiled=True)
    results = returned.reshape(local_experts, size_gy, CAP, result_width)
    expert_table = results.transpose(1, 0, 2, 3).reshape(EXPERTS * CAP, result_width)
    moe_output = jnp.dot(
        combine_table,
        expert_table,
        precision=lax.Precision.HIGHEST,
        preferred_element_type=jnp.float32,
    )
    return moe_output.astype(jnp.bfloat16)


def solution(mesh):
    return jax.shard_map(
        body,
        mesh=mesh,
        in_specs=(
            P(("gy", "gz"), "gx"),
            P(("gy", "gz"), None),
            P(("gy", "gz"), None),
            P("gy", None, ("gz", "gx")),
            P("gy", None, ("gz", "gx")),
            P("gy", "gz", "gx"),
        ),
        out_specs=P(("gy", "gz"), "gx"),
        check_vma=False,
    )
```

profile of v0, /device:TPU:2, one launch (start us, length us, event | category | flops | bytes accessed | tf_op | source)
XLA Modules:
  0.0 407.8 jit_solution(18347931550341492093)
XLA Ops:
  6.5 0.0 copy-start
  6.5 1.4 broadcast_in_dim.2
  8.0 0.0 copy-start.2
  8.0 26.0 %all-to-all-start = ((bf16[16,16,256]{2,1,0:T(8,128)(2,1)}), bf16[16,16,256]{2,1,0:T(8,128)(2,1)S(1)}, u32[]{:S(2)}, u32[]{:S(2)}) async-start(bf16[16,16,256]{2,1,0:T(8,128)(2,1)} %broadcast_in_dim.2), calls=%async_computation | async-start | bytes 262144 | tf_op jit(solution)/shard_map/all_to_all | solution.py:12
  34.0 0.0 all-gather.4.cloned.1.call-start
  34.0 0.8 copy.32
  34.8 0.1 eq.29
  34.9 0.1 fusion.7
  35.0 0.1 reduce_window_sum.11
  35.0 0.2 select_reduce_fusion.1
  35.2 0.1 reduce_sum.41
  35.3 0.1 copy.33
  35.4 0.7 multiply_add_fusion
  36.1 0.8 convert_reduce_fusion
  36.8 20.2 %all-to-all-done = bf16[16,16,256]{2,1,0:T(8,128)(2,1)S(1)} async-done(((bf16[16,16,256]{2,1,0:T(8,128)(2,1)}), bf16[16,16,256]{2,1,0:T(8,128)(2,1)S(1)}, u32[]{:S(2)}, u32[]{:S(2)}) %all-to-all-start) | async-done | bytes 131104 | tf_op jit(solution)/shard_map/all_to_all | solution.py:12
  57.0 0.3 fusion
  57.4 41.4 %all_to_all.20 = bf16[1,8,1,8,4096]{4,3,2,0,1:T(8,128)(2,1)} all-to-all(bf16[1,8,1,8,4096]{4,3,2,0,1:T(8,128)(2,1)S(1)} %fusion), channel_id=1, replica_groups=mesh['gx'=16,'gy'=8,'gz'=8] {'gy'}, dimensions={1} | all-to-all | bytes 1048576 | tf_op jit(solution)/shard_map/all_to_all | solution.py:71
  98.8 0.0 all-gather.4.cloned.1.call-update
  98.8 0.0 all-gather.6.cloned.1.call-start
  98.9 71.9 %all-gather.4.cloned.1.call-done = bf16[1,8,8,8,4096]{4,3,2,1,0:T(8,128)(2,1)} async-done(((bf16[1,8,1,8,4096]{4,3,2,1,0:T(8,128)(2,1)}), bf16[1,8,8,8,4096]{4,3,2,1,0:T(8,128)(2,1)}) %all-gather.4.cloned.1.call-update) | async-done | bytes 4194320 | tf_op jit(solution)/shard_map/all_gather | solution.py:72
  170.8 0.0 copy-start.1
  170.8 3.9 fusion.4
  174.6 0.0 copy-done.2
  174.7 0.0 copy-done.1
  174.7 1.9 fusion.1
  176.6 0.0 all-gather.6.cloned.1.call-update
  176.6 161.2 %all-gather.6.cloned.1.call-done = bf16[512,2048]{1,0:T(8,128)(2,1)} async-done(((bf16[512,128]{1,0:T(8,128)(2,1)}), bf16[512,2048]{1,0:T(8,128)(2,1)}) %all-gather.6.cloned.1.call-update) | async-done | bytes 2097168 | tf_op jit(solution)/shard_map/all_gather | solution.py:84
  337.8 0.0 copy-done
  337.8 2.3 convolution_bitcast_fusion
  340.1 14.0 %all_to_all.21 = f32[8,1,8,1,8,256]{5,4,2,3,1,0:T(8,128)S(1)} all-to-all(f32[8,1,8,1,8,256]{5,4,2,3,1,0:T(8,128)S(1)} %copy.37), channel_id=1, replica_groups=mesh['gx'=16,'gy'=8,'gz'=8] {'gz'}, dimensions={0} | all-to-all | bytes 1048576 | tf_op jit(solution)/shard_map/all_to_all | solution.py:36
  354.1 46.1 %all_to_all.22 = f32[1,8,1,8,256]{4,3,2,0,1:T(8,128)S(1)} all-to-all(f32[1,8,1,8,256]{4,3,2,0,1:T(8,128)S(1)} %bitcast.42), channel_id=1, replica_groups=mesh['gx'=16,'gy'=8,'gz'=8] {'gy'}, dimensions={1} | all-to-all | bytes 131072 | tf_op jit(solution)/shard_map/all_to_all | solution.py:90
  400.2 0.8 convolution_convert_fusion.1
  (3 shorter events, 0.1 us)
Async XLA Ops:
  6.5 331.3 %copy-start = (bf16[1,2048,256]{2,1,0:T(8,128)(2,1)S(1)}, bf16[1,2048,256]{2,1,0:T(8,128)(2,1)}, u32[]{:S(2)}) copy-start(bf16[1,2048,256]{2,1,0:T(8,128)(2,1)} %param.11) | copy-start | bytes 3145732
  8.0 166.7 %copy-start.2 = (bf16[1,4096,128]{2,1,0:T(8,128)(2,1)S(1)}, bf16[1,4096,128]{2,1,0:T(8,128)(2,1)}, u32[]{:S(2)}) copy-start(bf16[1,4096,128]{2,1,0:T(8,128)(2,1)} %param.10) | copy-start | bytes 3145732
  8.0 49.1 %all-to-all-start = ((bf16[16,16,256]{2,1,0:T(8,128)(2,1)}), bf16[16,16,256]{2,1,0:T(8,128)(2,1)S(1)}, u32[]{:S(2)}, u32[]{:S(2)}) async-start(bf16[16,16,256]{2,1,0:T(8,128)(2,1)} %broadcast_in_dim.2), calls=%async_computation | async-start | bytes 262144 | tf_op jit(solution)/shard_map/all_to_all | solution.py:12
  34.0 136.8 %all-gather.4.cloned.1.call-start = ((), (), s32[]{:S(2)}) async-start(), calls=%async_computation.4 | async-start | bytes 4718592 | tf_op jit(solution)/shard_map/all_gather | solution.py:72
  98.8 239.0 %all-gather.6.cloned.1.call-start = ((), (), s32[]{:S(2)}) async-start(), calls=%async_computation.5 | async-start | bytes 2228224 | tf_op jit(solution)/shard_map/all_gather | solution.py:84
  170.8 3.9 copy-start.1
Sparse Core Ops, SparseCore 0:
  98.9 71.7 all-gather.3
  176.7 161.0 all-gather.5
where the time goes:
time: 408 us
  waiting for transfers between devices  253 us (62%)
  blocking collectives  101 us (25%)
  starting transfers between devices  26.1 us (6%)
  between operations  13.5 us (3%)
  matrix products  9.15 us (2%)
    all_gather x1, waiting for transfers between devices, body(): lax.all_gather(hidden, 'gx', axis=2, tiled=True)  161 us
    all_gather x1, waiting for transfers between devices, body(): portion = lax.all_gather(arrived, 'gz', axis=2, tiled=True)  71.9 us
    all_to_all x1, blocking collectives, body(): lax.all_to_all(summed, 'gy', split_axis=1, concat_axis=1, tiled=True)  46.1 us
    all_to_all x1, blocking collectives, body(): lax.all_to_all(outgoing, 'gy', split_axis=1, concat_axis=1, tiled=True)  41.4 us
    all_to_all x1, starting transfers between devices, sent_to_all(): lax.all_to_all(jnp.broadcast_to(value[None], (count, *value.shape)), axis...  26 us
    all_to_all x1, waiting for transfers between devices, sent_to_all(): lax.all_to_all(jnp.broadcast_to(value[None], (count, *value.shape)), axis...  20.2 us
    all_to_all x1, blocking collectives, sum_at_owner(): lax.all_to_all(parts, axis, split_axis=0, concat_axis=0, tiled=True)  14 us
  transfers between devices with their start and end apart: 3, of which 3 were waited for; matrix products, arithmetic and copies ran while one was open for 1% of the time, Pallas kernels for 0%

commit v1 on v0

v1 whole, which is shorter than its diff:
```python
import jax
import jax.numpy as jnp
from jax import lax
from jax.sharding import Mesh, PartitionSpec as P


EXPERTS = 8
CAP = 8
BF = jnp.bfloat16
F32 = jnp.float32
AXES = ("gxh", "gxl", "zh", "y", "x", "c")
SIZES = (4, 4, 2, 4, 4, 2)


def sent_to_all(value, axis):
    count = lax.axis_size(axis)
    return lax.all_to_all(
        jnp.broadcast_to(value[None], (count, *value.shape)), axis, 0, 0, tiled=True
    )


def route_tables(expert_ids, gate_probs, experts, capacity):
    token_count = expert_ids.shape[0]
    flattened = expert_ids.reshape(token_count * 2)
    labels = jnp.arange(experts, dtype=jnp.int32)
    onehot = (flattened[:, None] == labels[None, :]).astype(jnp.int32)
    before = jnp.cumsum(onehot, axis=0) - onehot
    slot_index = jnp.sum(before * onehot, axis=1)
    places = flattened * capacity + slot_index
    columns = jnp.arange(experts * capacity, dtype=jnp.int32)
    matches = (places[:, None] == columns[None, :]).astype(F32)
    matches = matches.reshape(token_count, 2, experts * capacity)
    picker = jnp.sum(matches, axis=1)
    combine_table = jnp.sum(matches * gate_probs[:, :, None], axis=1)
    return (picker, combine_table)


def swiglu(rows, gate_weight, up_weight):
    gate = jnp.dot(rows, gate_weight, preferred_element_type=F32)
    up = jnp.dot(rows, up_weight, preferred_element_type=F32)
    return (jax.nn.silu(gate) * up).astype(BF)


def layer(tokens, expert_ids, gate_probs, gate_weight, up_weight, down_weight):
    near = lax.axis_index("gxl")
    gate_weight, up_weight, down_weight = gate_weight[0], up_weight[0], down_weight[0]
    width = tokens.shape[1]
    picker, combine_table = route_tables(expert_ids, gate_probs, EXPERTS, CAP)

    slots = jnp.einsum("tr,tf->rf", picker.astype(BF), tokens, preferred_element_type=F32)
    slots = slots.astype(BF).reshape(1, EXPERTS, CAP, width)
    outgoing = jnp.broadcast_to(slots, (4, EXPERTS, CAP, width)).reshape(-1, CAP, width)
    arrived = lax.all_to_all(outgoing, ("gxh", "zh", "y"), 0, 0, tiled=True)
    arrived = arrived.reshape(4, EXPERTS * CAP, width)

    joined = lax.all_gather(arrived, "gxl", axis=0, tiled=False)
    block = joined.transpose(2, 1, 0, 3).reshape(EXPERTS * CAP, 16 * width)

    block, down = lax.optimization_barrier((block, down_weight.reshape(4, 4, 128, width)))
    downs = []
    for shift in range(4):
        there = lax.bitwise_and(near + shift, 3)
        part = lax.dynamic_slice(down, (0, there, 0, 0), (4, 1, 128, width)).reshape(512, width)
        if shift:
            part = lax.ppermute(part, "gxl", [(i, (i + shift) % 4) for i in range(4)])
        downs.append(part)

    own = sent_to_all(block, "x").reshape(4 * EXPERTS * CAP, 16 * width)
    other = lax.ppermute(own, "c", [(0, 1), (1, 0)])

    hidden = jnp.concatenate(
        [swiglu(own, gate_weight, up_weight), swiglu(other, gate_weight, up_weight)], axis=0
    )
    hidden = lax.all_gather(hidden, "gxh", axis=1, tiled=True)

    half = hidden.shape[0] // 2
    parts_other = [jnp.dot(hidden[half:], w, preferred_element_type=F32).astype(BF) for w in downs]
    parts_own = [jnp.dot(hidden[:half], w, preferred_element_type=F32) for w in downs]
    received = lax.ppermute(jnp.stack(parts_other), "c", [(0, 1), (1, 0)])
    summed = jnp.stack(parts_own) + received.astype(F32)
    summed = summed.astype(BF).reshape(4, 4, EXPERTS * CAP, width).transpose(1, 0, 2, 3)
    summed = lax.all_to_all(summed, "x", 0, 0, tiled=True).astype(F32)
    place = jnp.arange(4, dtype=jnp.int32)
    order = (lax.bitwise_and(near - place[:, None], 3) == place[None, :]).astype(F32)
    placed = (order[:, None, :, None, None] * summed[None]).sum(axis=(1, 2))
    result = lax.all_to_all(placed.astype(BF), "gxl", 0, 0, tiled=True).astype(F32).sum(axis=0)

    result = result.astype(BF).reshape(EXPERTS, CAP, width)
    returned = lax.all_to_all(result, ("zh", "y"), 0, 0, tiled=True)
    table = returned.reshape(EXPERTS * CAP, width).astype(F32)
    out = jnp.dot(combine_table, table, precision=lax.Precision.HIGHEST, preferred_element_type=F32)
    return out.astype(BF)


def solution(mesh):
    split = Mesh(mesh.devices.reshape(SIZES), AXES)
    blocks, experts, hidden, features = ("zh", "y", "x", "c"), ("zh", "y"), ("x", "c"), ("gxh", "gxl")
    return jax.shard_map(
        layer,
        mesh=split,
        in_specs=(
            P(blocks, features),
            P(blocks, None),
            P(blocks, None),
            P(experts, None, hidden + features),
            P(experts, None, hidden + features),
            P(experts, hidden, features),
        ),
        out_specs=P(blocks, features),
        check_vma=False,
    )
```

time: 408 us -> 245 us (0.60)
  the two profiles are of different devices: /device:TPU:2 before, /device:TPU:32 now
where the time goes in v1:
time: 245 us
  blocking collectives  199 us (81%)
  starting transfers between devices  18.6 us (8%)
  waiting for transfers between devices  10.9 us (4%)
  matrix products  9.39 us (4%)
  local copies, waits for them, and re-layouts  4.25 us (2%)
  other arithmetic  2.5 us (1%)
    all_to_all x1, blocking collectives, layer(): arrived = lax.all_to_all(outgoing, ('gxh', 'zh', 'y'), 0, 0, tiled=True)  63 us
    all_gather x1, blocking collectives, layer(): hidden = lax.all_gather(hidden, 'gxh', axis=1, tiled=True)  54.9 us
    all_to_all x1, blocking collectives, layer(): returned = lax.all_to_all(result, ('zh', 'y'), 0, 0, tiled=True)  32.6 us
    all_to_all x1, blocking collectives, sent_to_all(): lax.all_to_all(jnp.broadcast_to(value[None], (count, *value.shape)), axis...  25.8 us
    all_gather x1, blocking collectives, layer(): joined = lax.all_gather(arrived, 'gxl', axis=0, tiled=False)  14.3 us
    ppermute x3, starting transfers between devices, layer(): part = lax.ppermute(part, 'gxl', [(i, (i + shift) % 4) for i in range(4)])  11.3 us
    all_to_all x1, waiting for transfers between devices, layer(): summed = lax.all_to_all(summed, 'x', 0, 0, tiled=True).astype(F32)  9.94 us
    all_to_all x1, blocking collectives, layer(): lax.all_to_all(placed.astype(BF), 'gxl', 0, 0, tiled=True).astype(F32)  8.26 us
  transfers between devices with their start and end apart: 6, of which 2 were waited for; matrix products, arithmetic and copies ran while one was open for 4% of the time, Pallas kernels for 0%

profile of v1, /device:TPU:32, one launch (start us, length us, event | category | flops | bytes accessed | tf_op | source)
XLA Modules:
  0.0 244.7 jit_solution(4071619516702738322)
XLA Ops:
  0.0 0.8 copy.35
  1.4 0.7 multiply_add_fusion
  2.1 0.8 convert_reduce_fusion
  2.9 0.9 fusion.5
  3.8 63.0 %all_to_all.25 = bf16[32,8,256]{2,1,0:T(8,128)(2,1)S(1)} all-to-all(bf16[32,8,256]{2,1,0:T(8,128)(2,1)S(1)} %bitcast.71), channel_id=1, replica_groups=mesh['gxh'=4,'gxl'=4,'zh'=2,'y'=4,'x'=4,'c'=2] {'gxh','zh','y'}, dimensions={0} | all-to-all | bytes 262144 | tf_op jit(solution)/shard_map/all_to_all | solution.py:53
  66.8 14.3 %all_gather.6 = bf16[4,4,64,256]{3,2,1,0:T(8,128)(2,1)S(1)} all-gather(bf16[1,4,64,256]{3,2,1,0:T(8,128)(2,1)S(1)} %bitcast.70), channel_id=1, replica_groups=mesh['gxh'=4,'gxl'=4,'zh'=2,'y'=4,'x'=4,'c'=2] {'gxl'}, dimensions={0}, use_global_device_ids=true | all-gather | bytes 655360 | tf_op jit(solution)/shard_map/all_gather | solution.py:56
  81.1 0.4 copy.37
  81.5 0.4 reshape.83
  81.9 0.2 broadcast_in_dim.8
  82.1 25.8 %all_to_all.26 = bf16[4,64,4096]{2,1,0:T(8,128)(2,1)S(1)} all-to-all(bf16[4,64,4096]{2,1,0:T(8,128)(2,1)S(1)} %broadcast_in_dim.8), channel_id=1, replica_groups=mesh['gxh'=4,'gxl'=4,'zh'=2,'y'=4,'x'=4,'c'=2] {'x'}, dimensions={0} | all-to-all | bytes 4194304 | tf_op jit(solution)/shard_map/all_to_all | solution.py:17
  107.9 1.9 collective-permute-start
  109.9 1.3 constant_dynamic-slice_fusion.2
  111.2 4.2 %collective-permute-start.3 = (bf16[512,256]{1,0:T(8,128)(2,1)S(1)}, bf16[512,256]{1,0:T(8,128)(2,1)S(1)}, u32[]{:S(2)}, u32[]{:S(2)}) collective-permute-start(bf16[512,256]{1,0:T(8,128)(2,1)S(1)} %bitcast.72), channel_id=1, source_target_pairs={{0,192},{64,0},{128,64},{192,128},{1,193},{65,1},{129,65},{193,129... | collective-permute-start | bytes 786440 | tf_op jit(solution)/shard_map/ppermute | solution.py:65
  115.4 2.8 %collective-permute-start.2 = (bf16[512,256]{1,0:T(8,128)(2,1)S(1)}, bf16[512,256]{1,0:T(8,128)(2,1)S(1)}, u32[]{:S(2)}, u32[]{:S(2)}) collective-permute-start(bf16[512,256]{1,0:T(8,128)(2,1)S(1)} %bitcast.73), channel_id=1, source_target_pairs={{0,128},{64,192},{128,0},{192,64},{1,129},{65,193},{129,1},{193,65... | collective-permute-start | bytes 786440 | tf_op jit(solution)/shard_map/ppermute | solution.py:65
  118.2 4.2 %collective-permute-start.1 = (bf16[512,256]{1,0:T(8,128)(2,1)S(1)}, bf16[512,256]{1,0:T(8,128)(2,1)S(1)}, u32[]{:S(2)}, u32[]{:S(2)}) collective-permute-start(bf16[512,256]{1,0:T(8,128)(2,1)S(1)} %bitcast.74), channel_id=1, source_target_pairs={{0,64},{64,128},{128,192},{192,0},{1,65},{65,129},{129,193},{193,1... | collective-permute-start | bytes 786440 | tf_op jit(solution)/shard_map/ppermute | solution.py:65
  122.5 0.7 fusion.12
  123.2 0.7 fusion.4
  123.9 2.3 fusion.10
  126.2 2.3 multiply_convert_fusion
  128.5 54.9 %all_gather.7 = bf16[512,512]{1,0:T(8,128)(2,1)S(1)} all-gather(bf16[512,128]{1,0:T(8,128)(2,1)S(1)} %pad_maximum_fusion.1), channel_id=1, replica_groups=mesh['gxh'=4,'gxl'=4,'zh'=2,'y'=4,'x'=4,'c'=2] {'gxh'}, dimensions={1}, use_global_device_ids=true | all-gather | bytes 655360 | tf_op jit(solution)/shard_map/all_gather | solution.py:74
  184.4 1.9 collective-permute-start.4
  186.5 0.2 convolution_bitcast_fusion.2
  186.8 0.2 convolution_bitcast_fusion.1
  187.0 0.2 convolution_bitcast_fusion
  187.3 0.9 collective-permute-done.4
  188.3 0.8 copy.40
  189.1 3.5 %all-to-all-start.2 = ((bf16[4,4,64,256]{3,2,1,0:T(8,128)(2,1)}), bf16[4,4,64,256]{3,2,1,0:T(8,128)(2,1)S(1)}, u32[]{:S(2)}, u32[]{:S(2)}) async-start(bf16[4,4,64,256]{3,2,1,0:T(8,128)(2,1)} %bitcast.61), calls=%async_computation.2 | async-start | bytes 1048576 | tf_op jit(solution)/shard_map/all_to_all | solution.py:82
  192.7 9.9 %all-to-all-done.2 = bf16[4,4,64,256]{3,2,1,0:T(8,128)(2,1)S(1)} async-done(((bf16[4,4,64,256]{3,2,1,0:T(8,128)(2,1)}), bf16[4,4,64,256]{3,2,1,0:T(8,128)(2,1)S(1)}, u32[]{:S(2)}, u32[]{:S(2)}) %all-to-all-start.2) | async-done | bytes 524320 | tf_op jit(solution)/shard_map/all_to_all | solution.py:82
  202.7 0.3 multiply_reduce_fusion
  203.1 8.3 %all_to_all.27 = bf16[4,64,256]{2,1,0:T(8,128)(2,1)S(1)} all-to-all(bf16[4,64,256]{2,1,0:T(8,128)(2,1)S(1)} %multiply_reduce_fusion), channel_id=1, replica_groups=mesh['gxh'=4,'gxl'=4,'zh'=2,'y'=4,'x'=4,'c'=2] {'gxl'}, dimensions={0} | all-to-all | bytes 262144 | tf_op jit(solution)/shard_map/all_to_all | solution.py:86
  211.4 32.6 %all_to_all.28 = bf16[8,8,256]{2,1,0:T(8,128)(2,1)S(1)} all-to-all(bf16[8,8,256]{2,1,0:T(8,128)(2,1)S(1)} %bitcast.75), channel_id=1, replica_groups=mesh['gxh'=4,'gxl'=4,'zh'=2,'y'=4,'x'=4,'c'=2] {'zh','y'}, dimensions={0} | all-to-all | bytes 65536 | tf_op jit(solution)/shard_map/all_to_all | solution.py:89
  243.9 0.7 convolution_convert_fusion.5
  (27 shorter events, 2.1 us)
Async XLA Ops:
  0.0 122.5 %copy-start = (bf16[1,4096,128]{2,1,0:T(8,128)(2,1)S(1)}, bf16[1,4096,128]{2,1,0:T(8,128)(2,1)}, u32[]{:S(2)}) copy-start(bf16[1,4096,128]{2,1,0:T(8,128)(2,1)} %param.9) | copy-start | bytes 3145732
  107.9 15.9 %collective-permute-start = (bf16[256,4096]{1,0:T(8,128)(2,1)S(1)}, bf16[256,4096]{1,0:T(8,128)(2,1)}, u32[]{:S(2)}, u32[]{:S(2)}) collective-permute-start(bf16[256,4096]{1,0:T(8,128)(2,1)S(1)} %bitcast.62), channel_id=1, source_target_pairs={{0,1},{1,0},{2,3},{3,2},{4,5},{5,4},{6,7},{7,6},{8,9},{9,8},{10,11... | collective-permute-start | bytes 6291464 | tf_op jit(solution)/shard_map/ppermute | solution.py:69
  111.2 12.0 %copy-start.1 = (bf16[1,4096,128]{2,1,0:T(8,128)(2,1)S(1)}, bf16[1,4096,128]{2,1,0:T(8,128)(2,1)}, u32[]{:S(2)}) copy-start(bf16[1,4096,128]{2,1,0:T(8,128)(2,1)} %param.10) | copy-start | bytes 3145732
  111.2 72.9 %collective-permute-start.3 = (bf16[512,256]{1,0:T(8,128)(2,1)S(1)}, bf16[512,256]{1,0:T(8,128)(2,1)S(1)}, u32[]{:S(2)}, u32[]{:S(2)}) collective-permute-start(bf16[512,256]{1,0:T(8,128)(2,1)S(1)} %bitcast.72), channel_id=1, source_target_pairs={{0,192},{64,0},{128,64},{192,128},{1,193},{65,1},{129,65},{193,129... | collective-permute-start | bytes 786440 | tf_op jit(solution)/shard_map/ppermute | solution.py:65
  115.4 68.4 %collective-permute-start.2 = (bf16[512,256]{1,0:T(8,128)(2,1)S(1)}, bf16[512,256]{1,0:T(8,128)(2,1)S(1)}, u32[]{:S(2)}, u32[]{:S(2)}) collective-permute-start(bf16[512,256]{1,0:T(8,128)(2,1)S(1)} %bitcast.73), channel_id=1, source_target_pairs={{0,128},{64,192},{128,0},{192,64},{1,129},{65,193},{129,1},{193,65... | collective-permute-start | bytes 786440 | tf_op jit(solution)/shard_map/ppermute | solution.py:65
  118.2 65.4 %collective-permute-start.1 = (bf16[512,256]{1,0:T(8,128)(2,1)S(1)}, bf16[512,256]{1,0:T(8,128)(2,1)S(1)}, u32[]{:S(2)}, u32[]{:S(2)}) collective-permute-start(bf16[512,256]{1,0:T(8,128)(2,1)S(1)} %bitcast.74), channel_id=1, source_target_pairs={{0,64},{64,128},{128,192},{192,0},{1,65},{65,129},{129,193},{193,1... | collective-permute-start | bytes 786440 | tf_op jit(solution)/shard_map/ppermute | solution.py:65
  184.4 3.8 %collective-permute-start.4 = (bf16[4,256,256]{2,1,0:T(8,128)(2,1)S(1)}, bf16[4,256,256]{2,1,0:T(8,128)(2,1)S(1)}, u32[]{:S(2)}, u32[]{:S(2)}) collective-permute-start(bf16[4,256,256]{2,1,0:T(8,128)(2,1)S(1)} %pad_maximum_fusion), channel_id=1, source_target_pairs={{0,1},{1,0},{2,3},{3,2},{4,5},{5,4},{6,7},{7,6},{8,9},{9,8},{10,11... | collective-permute-start | bytes 1572872 | tf_op jit(solution)/shard_map/ppermute | solution.py:79
  189.1 13.5 %all-to-all-start.2 = ((bf16[4,4,64,256]{3,2,1,0:T(8,128)(2,1)}), bf16[4,4,64,256]{3,2,1,0:T(8,128)(2,1)S(1)}, u32[]{:S(2)}, u32[]{:S(2)}) async-start(bf16[4,4,64,256]{3,2,1,0:T(8,128)(2,1)} %bitcast.61), calls=%async_computation.2 | async-start | bytes 1048576 | tf_op jit(solution)/shard_map/all_to_all | solution.py:82

commit v2 on v1

v2 whole, which is shorter than its diff:
```python
import jax
import jax.numpy as jnp
from jax import lax
from jax.experimental import pallas as pl
from jax.experimental.pallas import tpu as pltpu
from jax.sharding import Mesh, PartitionSpec as P


EXPERTS = 8
CAP = 8
BF = jnp.bfloat16
F32 = jnp.float32
AXES = ("gxh", "gxl", "zh", "y", "x", "c")
SIZES = (4, 4, 2, 4, 4, 2)


def sent_to_all(value, axis):
    count = lax.axis_size(axis)
    return lax.all_to_all(
        jnp.broadcast_to(value[None], (count, *value.shape)), axis, 0, 0, tiled=True
    )


def route_kernel(ids_ref, probs_ref, tokens_ref, slots_ref, table_ref):
    places, count = table_ref.shape
    row = lax.broadcasted_iota(jnp.int32, (places, count), 0)
    expert, slot = row // CAP, row % CAP
    first = expert == ids_ref[0:1, :]
    second = expert == ids_ref[1:2, :]
    named = first.astype(F32) + second.astype(F32)
    earlier = lax.broadcasted_iota(jnp.int32, (count, count), 0) < lax.broadcasted_iota(
        jnp.int32, (count, count), 1
    )
    before = jnp.dot(named.astype(BF), earlier.astype(F32).astype(BF), preferred_element_type=F32)
    at = slot.astype(F32)
    first = (first & (before == at)).astype(F32)
    second = (second & (before == at)).astype(F32)
    table_ref[...] = first * probs_ref[0:1, :] + second * probs_ref[1:2, :]
    picker = (first + second).astype(BF)
    rows = jnp.dot(picker, tokens_ref[...], preferred_element_type=F32).astype(BF)
    for copy in range(slots_ref.shape[0]):
        slots_ref[copy] = rows


def route(expert_ids, gate_probs, tokens, copies):
    count, width = tokens.shape
    return pl.pallas_call(
        route_kernel,
        out_shape=(
            jax.ShapeDtypeStruct((copies, EXPERTS * CAP, width), BF),
            jax.ShapeDtypeStruct((EXPERTS * CAP, count), F32),
        ),
        name="route",
    )(expert_ids.T, gate_probs.T, tokens)


def down_kernel(near_ref, hidden_ref, w0, w1, w2, w3, out_ref):
    hidden = hidden_ref[...]
    for shift, weight in enumerate((w0, w1, w2, w3)):
        part = jnp.dot(hidden, weight[...], preferred_element_type=F32)
        out_ref[lax.bitwise_and(near_ref[0] - shift, 3)] = part.astype(out_ref.dtype)


def down_projection(near, hidden, half, downs, dtype):
    rows, depth = hidden.shape[0] // 2, hidden.shape[1]
    width = downs[0].shape[1]
    whole = pl.BlockSpec((depth, width), lambda i, near: (0, 0))
    return pl.pallas_call(
        down_kernel,
        grid_spec=pltpu.PrefetchScalarGridSpec(
            num_scalar_prefetch=1,
            grid=(1,),
            in_specs=[pl.BlockSpec((rows, depth), lambda i, near: (half, 0))] + [whole] * 4,
            out_specs=pl.BlockSpec((4, rows, width), lambda i, near: (0, 0, 0)),
        ),
        out_shape=jax.ShapeDtypeStruct((4, rows, width), dtype),
        name="down",
    )(near, hidden, *downs)


def swiglu(rows, gate_weight, up_weight):
    gate = jnp.dot(rows, gate_weight, preferred_element_type=F32)
    up = jnp.dot(rows, up_weight, preferred_element_type=F32)
    return (jax.nn.silu(gate) * up).astype(BF)


def layer(tokens, expert_ids, gate_probs, gate_weight, up_weight, down_weight):
    near = lax.axis_index("gxl")
    gate_weight, up_weight, down_weight = gate_weight[0], up_weight[0], down_weight[0]
    width = tokens.shape[1]

    outgoing, combine_table = route(expert_ids, gate_probs, tokens, 4)
    outgoing = outgoing.reshape(-1, CAP, width)
    arrived = lax.all_to_all(outgoing, ("gxh", "zh", "y"), 0, 0, tiled=True)
    arrived = arrived.reshape(4, EXPERTS * CAP, width)

    joined = lax.all_gather(arrived, "gxl", axis=0, tiled=False)
    block = joined.transpose(2, 1, 0, 3).reshape(EXPERTS * CAP, 16 * width)

    block, down = lax.optimization_barrier((block, down_weight.reshape(4, 4, 128, width)))
    downs = []
    for shift in range(4):
        there = lax.bitwise_and(near + shift, 3)
        part = lax.dynamic_slice(down, (0, there, 0, 0), (4, 1, 128, width)).reshape(512, width)
        if shift:
            part = lax.ppermute(part, "gxl", [(i, (i + shift) % 4) for i in range(4)])
        downs.append(part)

    own = sent_to_all(block, "x").reshape(4 * EXPERTS * CAP, 16 * width)
    other = lax.ppermute(own, "c", [(0, 1), (1, 0)])

    hidden = jnp.concatenate(
        [swiglu(own, gate_weight, up_weight), swiglu(other, gate_weight, up_weight)], axis=0
    )
    hidden = lax.all_gather(hidden, "gxh", axis=1, tiled=True)

    place = near.reshape(1)
    for_other = down_projection(place, hidden, 1, downs, BF)
    summed = down_projection(place, hidden, 0, downs, F32)
    received = lax.ppermute(for_other, "c", [(0, 1), (1, 0)])
    summed = (summed + received.astype(F32)).astype(BF)
    summed = summed.reshape(16, EXPERTS * CAP, width)
    summed = lax.all_to_all(summed, ("gxl", "x"), 0, 0, tiled=True)
    result = summed.astype(F32).sum(axis=0)

    result = result.astype(BF).reshape(EXPERTS, CAP, width)
    returned = lax.all_to_all(result, ("zh", "y"), 0, 0, tiled=True)
    table = returned.reshape(EXPERTS * CAP, width).astype(F32)
    out = jnp.einsum(
        "rt,rf->tf",
        combine_table,
        table,
        precision=lax.Precision.HIGHEST,
        preferred_element_type=F32,
    )
    return out.astype(BF)


def solution(mesh):
    split = Mesh(mesh.devices.reshape(SIZES), AXES)
    blocks, experts, hidden, features = ("zh", "y", "x", "c"), ("zh", "y"), ("x", "c"), ("gxh", "gxl")
    return jax.shard_map(
        layer,
        mesh=split,
        in_specs=(
            P(blocks, features),
            P(blocks, None),
            P(blocks, None),
            P(experts, None, hidden + features),
            P(experts, None, hidden + features),
            P(experts, hidden, features),
        ),
        out_specs=P(blocks, features),
        check_vma=False,
    )
```

time: 245 us -> 244 us (level)
  blocking collectives: 199 us -> 210 us
  waiting for transfers between devices: 10.9 us -> 0.01 us
  Pallas kernels: 0 us -> 6.9 us
  starting transfers between devices: 18.6 us -> 14.2 us
  matrix products: 9.39 us -> 6.76 us
    all_to_all x1, blocking collectives: 8.26 us -> 23.9 us  [layer(): summed = lax.all_to_all(summed, ('gxl', 'x'), 0, 0, tiled=True)]
    all_to_all x1 -> x0, waiting for transfers between devices: 9.94 us -> none  [layer(): summed = lax.all_to_all(summed, 'x', 0, 0, tiled=True).astype(F32)]
    pallas_call x0 -> x3, Pallas kernels: none -> 6.9 us  [the longest x2 5.18 us: down_projection(): pl.pallas_call(down_kernel, grid_spec=pltpu.PrefetchScalarGridSpec(num_sc...]
    all_gather x1, blocking collectives: 54.9 us -> 50.3 us  [layer(): hidden = lax.all_gather(hidden, 'gxh', axis=1, tiled=True)]
    all_to_all x1 -> x0, starting transfers between devices: 3.47 us -> none  [layer(): summed = lax.all_to_all(summed, 'x', 0, 0, tiled=True).astype(F32)]
    dot_general x10 -> x1, matrix products: 3.43 us -> 0.8 us  [layer(): jnp.einsum('rt,rf->tf', combine_table, table, precision=lax.Precision.HIG...]
  transfers between devices with their start and end apart: 6 -> 5, of which waited for: 2 -> 0; matrix products, arithmetic and copies ran while one was open for 4% -> 3% of each run, Pallas kernels for 0% -> 1%
where the time goes in v2:
time: 244 us; the launch traced here: 243 us
  blocking collectives  210 us (86%)
  starting transfers between devices  14.2 us (6%)
  Pallas kernels  6.9 us (3%)
  matrix products  6.76 us (3%)
  local copies, waits for them, and re-layouts  3.73 us (2%)
    all_to_all x1, blocking collectives, layer(): arrived = lax.all_to_all(outgoing, ('gxh', 'zh', 'y'), 0, 0, tiled=True)  63.2 us
    all_gather x1, blocking collectives, layer(): hidden = lax.all_gather(hidden, 'gxh', axis=1, tiled=True)  50.3 us
    all_to_all x1, blocking collectives, layer(): returned = lax.all_to_all(result, ('zh', 'y'), 0, 0, tiled=True)  32.7 us
    all_to_all x1, blocking collectives, sent_to_all(): lax.all_to_all(jnp.broadcast_to(value[None], (count, *value.shape)), axis...  25.8 us
    all_to_all x1, blocking collectives, layer(): summed = lax.all_to_all(summed, ('gxl', 'x'), 0, 0, tiled=True)  23.9 us
    all_gather x1, blocking collectives, layer(): joined = lax.all_gather(arrived, 'gxl', axis=0, tiled=False)  14.3 us
    ppermute x3, starting transfers between devices, layer(): part = lax.ppermute(part, 'gxl', [(i, (i + shift) % 4) for i in range(4)])  10.4 us
    pallas_call x2, Pallas kernels, down_projection(): pl.pallas_call(down_kernel, grid_spec=pltpu.PrefetchScalarGridSpec(num_sc...  5.18 us
  transfers between devices with their start and end apart: 5, of which 0 were waited for; matrix products, arithmetic and copies ran while one was open for 3% of the time, Pallas kernels for 1%

profile of v2, /device:TPU:32, one launch (start us, length us, event | category | flops | bytes accessed | tf_op | source)
XLA Modules:
  0.0 243.4 jit_solution(18124636227922163590)
XLA Ops:
  0.0 0.0 copy-start
  0.0 1.7 route.1
  1.7 63.2 %all_to_all.20 = bf16[32,8,256]{2,1,0:T(8,128)(2,1)S(1)} all-to-all(bf16[32,8,256]{2,1,0:T(8,128)(2,1)} %bitcast.47), channel_id=1, replica_groups=mesh['gxh'=4,'gxl'=4,'zh'=2,'y'=4,'x'=4,'c'=2] {'gxh','zh','y'}, dimensions={0} | all-to-all | bytes 262144 | tf_op jit(solution)/shard_map/all_to_all | solution.py:94
  64.9 14.3 %all_gather.6 = bf16[4,4,64,256]{3,2,1,0:T(8,128)(2,1)S(1)} all-gather(bf16[1,4,64,256]{3,2,1,0:T(8,128)(2,1)S(1)} %bitcast.42), channel_id=1, replica_groups=mesh['gxh'=4,'gxl'=4,'zh'=2,'y'=4,'x'=4,'c'=2] {'gxl'}, dimensions={0}, use_global_device_ids=true | all-gather | bytes 655360 | tf_op jit(solution)/shard_map/all_gather | solution.py:97
  79.3 0.4 copy.20
  79.7 0.4 reshape.36
  80.0 0.2 broadcast_in_dim.2
  80.3 25.8 %all_to_all.21 = bf16[4,64,4096]{2,1,0:T(8,128)(2,1)S(1)} all-to-all(bf16[4,64,4096]{2,1,0:T(8,128)(2,1)S(1)} %broadcast_in_dim.2), channel_id=1, replica_groups=mesh['gxh'=4,'gxl'=4,'zh'=2,'y'=4,'x'=4,'c'=2] {'x'}, dimensions={0} | all-to-all | bytes 4194304 | tf_op jit(solution)/shard_map/all_to_all | solution.py:19
  106.1 1.9 collective-permute-start
  108.0 2.0 constant_dynamic-slice_fusion
  110.0 3.6 %collective-permute-start.1 = (bf16[512,256]{1,0:T(8,128)(2,1)S(1)}, bf16[512,256]{1,0:T(8,128)(2,1)S(1)}, u32[]{:S(2)}, u32[]{:S(2)}) collective-permute-start(bf16[512,256]{1,0:T(8,128)(2,1)S(1)} %bitcast.45), channel_id=1, source_target_pairs={{0,64},{64,128},{128,192},{192,0},{1,65},{65,129},{129,193},{193,1... | collective-permute-start | bytes 786440 | tf_op jit(solution)/shard_map/ppermute | solution.py:106
  113.6 4.9 %collective-permute-start.2 = (bf16[512,256]{1,0:T(8,128)(2,1)S(1)}, bf16[512,256]{1,0:T(8,128)(2,1)}, u32[]{:S(2)}, u32[]{:S(2)}) collective-permute-start(bf16[512,256]{1,0:T(8,128)(2,1)S(1)} %bitcast.44), channel_id=1, source_target_pairs={{0,128},{64,192},{128,0},{192,64},{1,129},{65,193},{129,1},{193,65... | collective-permute-start | bytes 786440 | tf_op jit(solution)/shard_map/ppermute | solution.py:106
  118.5 1.9 collective-permute-start.3
  120.4 0.7 fusion.6
  121.2 0.7 fusion
  121.9 0.0 collective-permute-done
  121.9 2.3 fusion.4
  124.2 2.3 multiply_convert_fusion
  126.5 50.3 %all_gather.7.hidden_ref = bf16[512,512]{1,0:T(8,128)(2,1)} all-gather(bf16[512,128]{1,0:T(8,128)(2,1)S(1)} %pad_maximum_fusion), channel_id=1, replica_groups=mesh['gxh'=4,'gxl'=4,'zh'=2,'y'=4,'x'=4,'c'=2] {'gxh'}, dimensions={1}, use_global_device_ids=true | all-gather | bytes 655360 | tf_op jit(solution)/shard_map/all_gather | solution.py:115
  176.8 0.0 collective-permute-done.1.w1
  176.8 0.0 collective-permute-done.2.w2
  176.8 0.0 collective-permute-done.3.w3
  176.8 0.7 copy-done.1
  177.5 2.5 %down.3 = bf16[4,256,256]{2,1,0:T(8,128)(2,1)} custom-call(s32[1]{0:T(128)} %bitcast.2.near_ref, bf16[512,512]{1,0:T(8,128)(2,1)} %all_gather.7.hidden_ref, bf16[512,256]{1,0:T(8,128)(2,1)} %bitcast.37, bf16[512,256]{1,0:T(8,128)(2,1)} %copy-done.1, bf16[512,256]{1,0:T(8,128)(2,1)} %collective-permute-done.2.w2, bf16[512,256]{1,0:T(8,128)(2,1)} %collective-permute-done.3.w3), custom_call_target="tpu_custom_call" | custom-call | tf_op jit(solution)/shard_map/down/pallas_call | solution.py:68
  180.0 1.9 collective-permute-start.4
  181.9 2.7 %down.2 = f32[4,256,256]{2,1,0:T(8,128)} custom-call(s32[1]{0:T(128)} %bitcast.2.near_ref, bf16[512,512]{1,0:T(8,128)(2,1)} %all_gather.7.hidden_ref, bf16[512,256]{1,0:T(8,128)(2,1)} %bitcast.38, bf16[512,256]{1,0:T(8,128)(2,1)} %copy-done.1, bf16[512,256]{1,0:T(8,128)(2,1)} %collective-permute-done.2.w2, bf16[512,256]{1,0:T(8,128)(2,1)} %collective-permute-done.3.w3), custom_call_target="tpu_custom_call" | custom-call | tf_op jit(solution)/shard_map/down/pallas_call | solution.py:68
  184.6 0.0 collective-permute-done.4
  184.6 1.4 add_convert_fusion
  186.0 23.9 %all_to_all.22 = bf16[16,64,256]{2,1,0:T(8,128)(2,1)S(1)} all-to-all(bf16[16,64,256]{2,1,0:T(8,128)(2,1)S(1)} %bitcast.40), channel_id=1, replica_groups=mesh['gxh'=4,'gxl'=4,'zh'=2,'y'=4,'x'=4,'c'=2] {'gxl','x'}, dimensions={0} | all-to-all | bytes 1048576 | tf_op jit(solution)/shard_map/all_to_all | solution.py:123
  209.8 0.1 reduce_sum.12
  209.9 32.7 %all_to_all.23 = bf16[8,8,256]{2,1,0:T(8,128)(2,1)S(1)} all-to-all(bf16[8,8,256]{2,1,0:T(8,128)(2,1)S(1)} %bitcast.46), channel_id=1, replica_groups=mesh['gxh'=4,'gxl'=4,'zh'=2,'y'=4,'x'=4,'c'=2] {'zh','y'}, dimensions={0} | all-to-all | bytes 65536 | tf_op jit(solution)/shard_map/all_to_all | solution.py:127
  242.6 0.8 convolution_convert_fusion
  (7 shorter events, 0.0 us)
Async XLA Ops:
  0.0 120.4 %copy-start = (bf16[1,4096,128]{2,1,0:T(8,128)(2,1)S(1)}, bf16[1,4096,128]{2,1,0:T(8,128)(2,1)}, u32[]{:S(2)}) copy-start(bf16[1,4096,128]{2,1,0:T(8,128)(2,1)} %param.9) | copy-start | bytes 3145732
  106.1 15.8 %collective-permute-start = (bf16[256,4096]{1,0:T(8,128)(2,1)S(1)}, bf16[256,4096]{1,0:T(8,128)(2,1)}, u32[]{:S(2)}, u32[]{:S(2)}) collective-permute-start(bf16[256,4096]{1,0:T(8,128)(2,1)S(1)} %bitcast.34), channel_id=1, source_target_pairs={{0,1},{1,0},{2,3},{3,2},{4,5},{5,4},{6,7},{7,6},{8,9},{9,8},{10,11... | collective-permute-start | bytes 6291464 | tf_op jit(solution)/shard_map/ppermute | solution.py:110
  110.0 11.1 %copy-start.3 = (bf16[1,4096,128]{2,1,0:T(8,128)(2,1)S(1)}, bf16[1,4096,128]{2,1,0:T(8,128)(2,1)}, u32[]{:S(2)}) copy-start(bf16[1,4096,128]{2,1,0:T(8,128)(2,1)} %param.10) | copy-start | bytes 3145732
  110.0 66.8 %collective-permute-start.1 = (bf16[512,256]{1,0:T(8,128)(2,1)S(1)}, bf16[512,256]{1,0:T(8,128)(2,1)S(1)}, u32[]{:S(2)}, u32[]{:S(2)}) collective-permute-start(bf16[512,256]{1,0:T(8,128)(2,1)S(1)} %bitcast.45), channel_id=1, source_target_pairs={{0,64},{64,128},{128,192},{192,0},{1,65},{65,129},{129,193},{193,1... | collective-permute-start | bytes 786440 | tf_op jit(solution)/shard_map/ppermute | solution.py:106
  113.6 63.2 %collective-permute-start.2 = (bf16[512,256]{1,0:T(8,128)(2,1)S(1)}, bf16[512,256]{1,0:T(8,128)(2,1)}, u32[]{:S(2)}, u32[]{:S(2)}) collective-permute-start(bf16[512,256]{1,0:T(8,128)(2,1)S(1)} %bitcast.44), channel_id=1, source_target_pairs={{0,128},{64,192},{128,0},{192,64},{1,129},{65,193},{129,1},{193,65... | collective-permute-start | bytes 786440 | tf_op jit(solution)/shard_map/ppermute | solution.py:106
  118.5 58.3 %collective-permute-start.3 = (bf16[512,256]{1,0:T(8,128)(2,1)S(1)}, bf16[512,256]{1,0:T(8,128)(2,1)}, u32[]{:S(2)}, u32[]{:S(2)}) collective-permute-start(bf16[512,256]{1,0:T(8,128)(2,1)S(1)} %bitcast.43), channel_id=1, source_target_pairs={{0,192},{64,0},{128,64},{192,128},{1,193},{65,1},{129,65},{193,129... | collective-permute-start | bytes 786440 | tf_op jit(solution)/shard_map/ppermute | solution.py:106
  176.8 0.7 copy-start.1
  180.0 4.6 %collective-permute-start.4 = (bf16[4,256,256]{2,1,0:T(8,128)(2,1)}, bf16[4,256,256]{2,1,0:T(8,128)(2,1)S(1)}, u32[]{:S(2)}, u32[]{:S(2)}) collective-permute-start(bf16[4,256,256]{2,1,0:T(8,128)(2,1)} %down.3), channel_id=1, source_target_pairs={{0,1},{1,0},{2,3},{3,2},{4,5},{5,4},{6,7},{7,6},{8,9},{9,8},{10,11... | collective-permute-start | bytes 1572872 | tf_op jit(solution)/shard_map/ppermute | solution.py:120
  184.6 58.0 %copy-start.2 = (f32[64,16]{1,0:T(8,128)S(1)}, f32[64,16]{1,0:T(8,128)}, u32[]{:S(2)}) copy-start(f32[64,16]{1,0:T(8,128)} %get-tuple-element.9) | copy-start | bytes 12292

commit v3 on v2

--- a/solution.py
+++ b/solution.py
@@ -2,7 +2,6 @@
 import jax.numpy as jnp
 from jax import lax
 from jax.experimental import pallas as pl
-from jax.experimental.pallas import tpu as pltpu
 from jax.sharding import Mesh, PartitionSpec as P
 
 
@@ -54,30 +53,6 @@
     )(expert_ids.T, gate_probs.T, tokens)
 
 
-def down_kernel(near_ref, hidden_ref, w0, w1, w2, w3, out_ref):
-    hidden = hidden_ref[...]
-    for shift, weight in enumerate((w0, w1, w2, w3)):
-        part = jnp.dot(hidden, weight[...], preferred_element_type=F32)
-        out_ref[lax.bitwise_and(near_ref[0] - shift, 3)] = part.astype(out_ref.dtype)
-
-
-def down_projection(near, hidden, half, downs, dtype):
-    rows, depth = hidden.shape[0] // 2, hidden.shape[1]
-    width = downs[0].shape[1]
-    whole = pl.BlockSpec((depth, width), lambda i, near: (0, 0))
-    return pl.pallas_call(
-        down_kernel,
-        grid_spec=pltpu.PrefetchScalarGridSpec(
-            num_scalar_prefetch=1,
-            grid=(1,),
-            in_specs=[pl.BlockSpec((rows, depth), lambda i, near: (half, 0))] + [whole] * 4,
-            out_specs=pl.BlockSpec((4, rows, width), lambda i, near: (0, 0, 0)),
-        ),
-        out_shape=jax.ShapeDtypeStruct((4, rows, width), dtype),
-        name="down",
-    )(near, hidden, *downs)
-
-
 def swiglu(rows, gate_weight, up_weight):
     gate = jnp.dot(rows, gate_weight, preferred_element_type=F32)
     up = jnp.dot(rows, up_weight, preferred_element_type=F32)
@@ -97,7 +72,7 @@
     joined = lax.all_gather(arrived, "gxl", axis=0, tiled=False)
     block = joined.transpose(2, 1, 0, 3).reshape(EXPERTS * CAP, 16 * width)
 
-    block, down = lax.optimization_barrier((block, down_weight.reshape(4, 4, 128, width)))
+    down = down_weight.reshape(4, 4, 128, width)
     downs = []
     for shift in range(4):
         there = lax.bitwise_and(near + shift, 3)
@@ -112,27 +87,44 @@
     hidden = jnp.concatenate(
         [swiglu(own, gate_weight, up_weight), swiglu(other, gate_weight, up_weight)], axis=0
     )
-    hidden = lax.all_gather(hidden, "gxh", axis=1, tiled=True)
+    hidden = lax.all_gather(hidden, "gxh", axis=0, tiled=False, axis_index_groups=[[0, 2, 3, 1]])
+    hidden = jnp.concatenate([hidden[j] for j in (0, 3, 1, 2)], axis=1)
 
-    place = near.reshape(1)
-    for_other = down_projection(place, hidden, 1, downs, BF)
-    summed = down_projection(place, hidden, 0, downs, F32)
-    received = lax.ppermute(for_other, "c", [(0, 1), (1, 0)])
-    summed = (summed + received.astype(F32)).astype(BF)
-    summed = summed.reshape(16, EXPERTS * CAP, width)
-    summed = lax.all_to_all(summed, ("gxl", "x"), 0, 0, tiled=True)
-    result = summed.astype(F32).sum(axis=0)
+    half = hidden.shape[0] // 2
+    hidden, downs = lax.optimization_barrier((hidden, downs))
+    downs = lax.optimization_barrier(jnp.stack(downs))
+    downs = [downs[shift] for shift in range(4)]
+    for_other = [jnp.dot(hidden[half:], w, preferred_element_type=F32) for w in downs]
+    own = [jnp.dot(hidden[:half], w, preferred_element_type=F32) for w in downs]
+    received = lax.ppermute(jnp.stack(for_other).astype(BF), "c", [(0, 1), (1, 0)])
+    place = jnp.arange(4, dtype=jnp.int32)
+    order = (lax.bitwise_and(near - place[:, None], 3) == place[None, :]).astype(F32)
+    summed = jnp.stack(own) + received.astype(F32)
+    summed = (order[:, :, None, None] * summed[None]).sum(axis=1).astype(BF)
+    summed = summed.reshape(4, 4, 2, 4, CAP, width).transpose(0, 3, 1, 2, 4, 5)
+    summed = summed.reshape(64, 2 * CAP, width)
+    summed = lax.all_to_all(summed, ("gxl", "y", "x"), 0, 0, tiled=True)
+    summed = summed.reshape(4, 4, 4, 2, CAP, width).astype(F32).sum(axis=(0, 2))
 
-    result = result.astype(BF).reshape(EXPERTS, CAP, width)
-    returned = lax.all_to_all(result, ("zh", "y"), 0, 0, tiled=True)
-    table = returned.reshape(EXPERTS * CAP, width).astype(F32)
-    out = jnp.einsum(
-        "rt,rf->tf",
-        combine_table,
-        table,
-        precision=lax.Precision.HIGHEST,
-        preferred_element_type=F32,
-    )
+    upper = lax.axis_index("zh") == 1
+    lows, highs = summed[:, 0], summed[:, 1]
+    kept = jnp.where(upper, highs, lows).reshape(4 * CAP, width)
+    sent = jnp.where(upper, lows, highs).astype(BF).reshape(4 * CAP, width)
+    got = lax.ppermute(sent, "zh", [(0, 1), (1, 0)]).astype(F32)
+    low_table, high_table = combine_table[: 4 * CAP], combine_table[4 * CAP :]
+    here = jnp.where(upper, high_table, low_table)
+    there = jnp.where(upper, low_table, high_table)
+
+    def mixed(table, values):
+        return jnp.einsum(
+            "rt,rf->tf",
+            table,
+            values,
+            precision=lax.Precision.HIGHEST,
+            preferred_element_type=F32,
+        )
+
+    out = mixed(here, kept) + mixed(there, got)
     return out.astype(BF)
 
 

time: 244 us -> 236 us (0.967)
  the two profiles are of different devices: /device:TPU:32 before, /device:TPU:2 now
where the time goes in v3:
time: 236 us; the launch traced here: 235 us
  blocking collectives  147 us (62%)
  starting transfers between devices  47.1 us (20%)
  waiting for transfers between devices  25.9 us (11%)
  matrix products  8.78 us (4%)
  local copies, waits for them, and re-layouts  3.2 us (1%)
    all_to_all x1, blocking collectives, layer(): arrived = lax.all_to_all(outgoing, ('gxh', 'zh', 'y'), 0, 0, tiled=True)  63.5 us
    all_gather x1, blocking collectives, layer(): lax.all_gather(hidden, 'gxh', axis=0, tiled=False, axis_index_groups=[[0,...  42.7 us
    all_to_all x1, blocking collectives, sent_to_all(): lax.all_to_all(jnp.broadcast_to(value[None], (count, *value.shape)), axis...  25.1 us
    all_to_all x1, starting transfers between devices, layer(): summed = lax.all_to_all(summed, ('gxl', 'y', 'x'), 0, 0, tiled=True)  17.5 us
    all_to_all x1, waiting for transfers between devices, layer(): summed = lax.all_to_all(summed, ('gxl', 'y', 'x'), 0, 0, tiled=True)  17.3 us
    ppermute x1, starting transfers between devices, layer(): got = lax.ppermute(sent, 'zh', [(0, 1), (1, 0)]).astype(F32)  16 us
    all_gather x1, blocking collectives, layer(): joined = lax.all_gather(arrived, 'gxl', axis=0, tiled=False)  15.9 us
    ppermute x3, starting transfers between devices, layer(): part = lax.ppermute(part, 'gxl', [(i, (i + shift) % 4) for i in range(4)])  9.69 us
  transfers between devices with their start and end apart: 7, of which 3 were waited for; matrix products, arithmetic and copies ran while one was open for 4% of the time, Pallas kernels for 0%

profile of v3, /device:TPU:2, one launch (start us, length us, event | category | flops | bytes accessed | tf_op | source)
XLA Modules:
  0.0 235.1 jit_solution(12365427514555121532)
XLA Ops:
  0.0 1.7 route.1
  1.7 63.5 %all_to_all.15 = bf16[32,8,256]{2,1,0:T(8,128)(2,1)S(1)} all-to-all(bf16[32,8,256]{2,1,0:T(8,128)(2,1)} %bitcast.90), channel_id=1, replica_groups=mesh['gxh'=4,'gxl'=4,'zh'=2,'y'=4,'x'=4,'c'=2] {'gxh','zh','y'}, dimensions={0} | all-to-all | bytes 262144 | tf_op jit(solution)/shard_map/all_to_all | solution.py:69
  65.2 15.9 %all_gather.9 = bf16[4,4,64,256]{3,2,1,0:T(8,128)(2,1)S(1)} all-gather(bf16[1,4,64,256]{3,2,1,0:T(8,128)(2,1)S(1)} %bitcast.83), channel_id=1, replica_groups=mesh['gxh'=4,'gxl'=4,'zh'=2,'y'=4,'x'=4,'c'=2] {'gxl'}, dimensions={0}, use_global_device_ids=true | all-gather | bytes 655360 | tf_op jit(solution)/shard_map/all_gather | solution.py:72
  81.1 0.4 copy.11
  81.5 0.4 broadcast_in_dim.4
  81.9 0.2 broadcast_in_dim.5
  82.1 25.1 %all_to_all.16 = bf16[4,64,4096]{2,1,0:T(8,128)(2,1)S(1)} all-to-all(bf16[4,64,4096]{2,1,0:T(8,128)(2,1)S(1)} %broadcast_in_dim.5), channel_id=1, replica_groups=mesh['gxh'=4,'gxl'=4,'zh'=2,'y'=4,'x'=4,'c'=2] {'x'}, dimensions={0} | all-to-all | bytes 4194304 | tf_op jit(solution)/shard_map/all_to_all | solution.py:18
  107.2 1.9 collective-permute-start
  109.2 1.3 constant_dynamic-slice_fusion
  110.5 2.1 collective-permute-start.1
  112.5 4.2 %collective-permute-start.2 = (bf16[512,256]{1,0:T(8,128)(2,1)S(1)}, bf16[512,256]{1,0:T(8,128)(2,1)S(1)}, u32[]{:S(2)}, u32[]{:S(2)}) collective-permute-start(bf16[512,256]{1,0:T(8,128)(2,1)S(1)} %bitcast.85), channel_id=1, source_target_pairs={{0,128},{64,192},{128,0},{192,64},{1,129},{65,193},{129,1},{193,65... | collective-permute-start | bytes 786440 | tf_op jit(solution)/shard_map/ppermute | solution.py:81
  116.7 3.4 %collective-permute-start.3 = (bf16[512,256]{1,0:T(8,128)(2,1)S(1)}, bf16[512,256]{1,0:T(8,128)(2,1)S(1)}, u32[]{:S(2)}, u32[]{:S(2)}) collective-permute-start(bf16[512,256]{1,0:T(8,128)(2,1)S(1)} %bitcast.84), channel_id=1, source_target_pairs={{0,192},{64,0},{128,64},{192,128},{1,193},{65,1},{129,65},{193,129... | collective-permute-start | bytes 786440 | tf_op jit(solution)/shard_map/ppermute | solution.py:81
  120.3 0.7 fusion.11
  121.0 0.7 fusion.4
  121.7 2.3 fusion.9
  124.0 2.3 multiply_convert_fusion
  126.3 42.7 %all-gather = bf16[2048,128]{1,0:T(8,128)(2,1)S(1)} all-gather(bf16[512,128]{1,0:T(8,128)(2,1)S(1)} %pad_maximum_fusion.3), channel_id=2, replica_groups={{0,512,768,256},{1,513,769,257},{2,514,770,258},{3,515,771,259},{4,516,..., dimensions={0}, use_global_device_ids=true | all-gather | bytes 655360 | tf_op jit(solution)/shard_map/all_gather | solution.py:90
  169.3 0.2 fusion.3
  169.5 0.2 fusion.2
  169.7 0.2 fusion.1
  170.0 0.2 fusion
  170.3 2.0 collective-permute-start.4
  172.5 0.2 convolution_bitcast_fusion.1
  172.8 0.2 convolution_bitcast_fusion.2
  173.3 0.8 collective-permute-done.4
  174.2 0.4 multiply_reduce_fusion
  174.6 0.9 copy.12
  175.5 17.5 %all-to-all-start.2 = ((bf16[64,16,256]{2,1,0:T(8,128)(2,1)}), bf16[64,16,256]{2,1,0:T(8,128)(2,1)S(1)}, u32[]{:S(2)}, u32[]{:S(2)}) async-start(bf16[64,16,256]{2,1,0:T(8,128)(2,1)} %bitcast.31), calls=%async_computation.2 | async-start | bytes 1048576 | tf_op jit(solution)/shard_map/all_to_all | solution.py:106
  192.9 17.3 %all-to-all-done.2 = bf16[64,16,256]{2,1,0:T(8,128)(2,1)S(1)} async-done(((bf16[64,16,256]{2,1,0:T(8,128)(2,1)}), bf16[64,16,256]{2,1,0:T(8,128)(2,1)S(1)}, u32[]{:S(2)}, u32[]{:S(2)}) %all-to-all-start.2) | async-done | bytes 524320 | tf_op jit(solution)/shard_map/all_to_all | solution.py:106
  210.3 16.0 %collective-permute-start.5 = (bf16[32,256]{1,0:T(8,128)(2,1)S(1)}, bf16[32,256]{1,0:T(8,128)(2,1)S(1)}, u32[]{:S(2)}, u32[]{:S(2)}) collective-permute-start(bf16[32,256]{1,0:T(8,128)(2,1)S(1)} %fusion.26), channel_id=1, source_target_pairs={{0,32},{32,0},{1,33},{33,1},{2,34},{34,2},{3,35},{35,3},{4,36},{36... | collective-permute-start | bytes 49160 | tf_op jit(solution)/shard_map/ppermute | solution.py:113
  226.6 7.7 %collective-permute-done.5 = bf16[32,256]{1,0:T(8,128)(2,1)S(1)} collective-permute-done((bf16[32,256]{1,0:T(8,128)(2,1)S(1)}, bf16[32,256]{1,0:T(8,128)(2,1)S(1)}, u32[]{:S(2)}, u32[]{:S(2)}) %collective-permute-start.5) | collective-permute-done | bytes 16416 | tf_op jit(solution)/shard_map/ppermute | solution.py:113
  234.3 0.8 fusion.5
  (23 shorter events, 1.2 us)
Async XLA Ops:
  0.0 120.3 %copy-start = (bf16[1,4096,128]{2,1,0:T(8,128)(2,1)S(1)}, bf16[1,4096,128]{2,1,0:T(8,128)(2,1)}, u32[]{:S(2)}) copy-start(bf16[1,4096,128]{2,1,0:T(8,128)(2,1)} %param.9) | copy-start | bytes 3145732
  107.2 14.4 %collective-permute-start = (bf16[256,4096]{1,0:T(8,128)(2,1)S(1)}, bf16[256,4096]{1,0:T(8,128)(2,1)}, u32[]{:S(2)}, u32[]{:S(2)}) collective-permute-start(bf16[256,4096]{1,0:T(8,128)(2,1)S(1)} %bitcast.75), channel_id=1, source_target_pairs={{0,1},{1,0},{2,3},{3,2},{4,5},{5,4},{6,7},{7,6},{8,9},{9,8},{10,11... | collective-permute-start | bytes 6291464 | tf_op jit(solution)/shard_map/ppermute | solution.py:85
  110.4 10.5 %copy-start.2 = (bf16[1,4096,128]{2,1,0:T(8,128)(2,1)S(1)}, bf16[1,4096,128]{2,1,0:T(8,128)(2,1)}, u32[]{:S(2)}) copy-start(bf16[1,4096,128]{2,1,0:T(8,128)(2,1)} %param.10) | copy-start | bytes 3145732
  110.5 58.6 %collective-permute-start.1 = (bf16[512,256]{1,0:T(8,128)(2,1)S(1)}, bf16[512,256]{1,0:T(8,128)(2,1)S(1)}, u32[]{:S(2)}, u32[]{:S(2)}) collective-permute-start(bf16[512,256]{1,0:T(8,128)(2,1)S(1)} %bitcast.86), channel_id=1, source_target_pairs={{0,64},{64,128},{128,192},{192,0},{1,65},{65,129},{129,193},{193,1... | collective-permute-start | bytes 786440 | tf_op jit(solution)/shard_map/ppermute | solution.py:81
  112.5 56.6 %collective-permute-start.2 = (bf16[512,256]{1,0:T(8,128)(2,1)S(1)}, bf16[512,256]{1,0:T(8,128)(2,1)S(1)}, u32[]{:S(2)}, u32[]{:S(2)}) collective-permute-start(bf16[512,256]{1,0:T(8,128)(2,1)S(1)} %bitcast.85), channel_id=1, source_target_pairs={{0,128},{64,192},{128,0},{192,64},{1,129},{65,193},{129,1},{193,65... | collective-permute-start | bytes 786440 | tf_op jit(solution)/shard_map/ppermute | solution.py:81
  116.7 52.4 %collective-permute-start.3 = (bf16[512,256]{1,0:T(8,128)(2,1)S(1)}, bf16[512,256]{1,0:T(8,128)(2,1)S(1)}, u32[]{:S(2)}, u32[]{:S(2)}) collective-permute-start(bf16[512,256]{1,0:T(8,128)(2,1)S(1)} %bitcast.84), channel_id=1, source_target_pairs={{0,192},{64,0},{128,64},{192,128},{1,193},{65,1},{129,65},{193,129... | collective-permute-start | bytes 786440 | tf_op jit(solution)/shard_map/ppermute | solution.py:81
  170.3 3.8 %collective-permute-start.4 = (bf16[4,256,256]{2,1,0:T(8,128)(2,1)S(1)}, bf16[4,256,256]{2,1,0:T(8,128)(2,1)S(1)}, u32[]{:S(2)}, u32[]{:S(2)}) collective-permute-start(bf16[4,256,256]{2,1,0:T(8,128)(2,1)S(1)} %pad_maximum_fusion.2), channel_id=1, source_target_pairs={{0,1},{1,0},{2,3},{3,2},{4,5},{5,4},{6,7},{7,6},{8,9},{9,8},{10,11... | collective-permute-start | bytes 1572872 | tf_op jit(solution)/shard_map/ppermute | solution.py:99
  174.2 52.2 %copy-start.1 = (f32[64,16]{1,0:T(8,128)S(1)}, f32[64,16]{1,0:T(8,128)}, u32[]{:S(2)}) copy-start(f32[64,16]{1,0:T(8,128)} %get-tuple-element.12) | copy-start | bytes 12292
  175.5 34.8 %all-to-all-start.2 = ((bf16[64,16,256]{2,1,0:T(8,128)(2,1)}), bf16[64,16,256]{2,1,0:T(8,128)(2,1)S(1)}, u32[]{:S(2)}, u32[]{:S(2)}) async-start(bf16[64,16,256]{2,1,0:T(8,128)(2,1)} %bitcast.31), calls=%async_computation.2 | async-start | bytes 1048576 | tf_op jit(solution)/shard_map/all_to_all | solution.py:106
  210.3 24.0 %collective-permute-start.5 = (bf16[32,256]{1,0:T(8,128)(2,1)S(1)}, bf16[32,256]{1,0:T(8,128)(2,1)S(1)}, u32[]{:S(2)}, u32[]{:S(2)}) collective-permute-start(bf16[32,256]{1,0:T(8,128)(2,1)S(1)} %fusion.26), channel_id=1, source_target_pairs={{0,32},{32,0},{1,33},{33,1},{2,34},{34,2},{3,35},{35,3},{4,36},{36... | collective-permute-start | bytes 49160 | tf_op jit(solution)/shard_map/ppermute | solution.py:113
